TPU v7x, 32 devices: a whole 2x2x4 slice. The times are simulated.
32 devices in a mesh: lat: 16 (over z, y, x), lev: 2 (over core).
Axes of the slice: x: 2, y: 2, z: 4, core: 2. Of those that a mesh axis runs over, the one named last changes fastest.
Arguments:
- fields: float32 [160, 3, 16, 2560], P('lat', None, 'lev'), may hold values from 0.1 to 5
- lat_fraction: float32 [160], P('lat'), may hold values from 0 to 1
- lon_fraction: float32 [160], P('lat'), may hold values from 0 to 1
- lon_shift: int32 [160], P('lat'), may hold values from 0 to 2559
- departure_row: int32 [160], P('lat'), may hold values from 1 to 157, as said below
- extents: int32 [16, 2], P('lat'), may hold values from 1 to 4
Outputs:
- advected: float32 [160, 3, 16, 2560], P('lat', None, 'lev')
Inputs may be any that keep to these rules, and one draw needn't show every extreme that they name: departure_row[r] lies within 39 rows of r.
All inputs are finite; a program needn't handle non-finite values.
Results may differ from a plain program's by a relative error of at most 0.0003.
Values sent between devices are 32-bit elements; how exact they have to be, the bound alone decides.
A program may use at most 128 MiB of HBM per device.

v0:
```python
import math

import jax
import jax.numpy as jnp
from jax import lax
from jax.sharding import PartitionSpec as P

REACH = 4


def from_behind(block, axis, distance):
    devices = range(lax.axis_size(axis))
    route = [(i - distance, i) for i in devices if i - distance in devices]
    return lax.ppermute(block, axis, route)


def cubic_weights(fraction):
    return jnp.stack(
        [
            -fraction * (fraction - 1.0) * (fraction - 2.0) / 6.0,
            (fraction + 1.0) * (fraction - 1.0) * (fraction - 2.0) / 2.0,
            -(fraction + 1.0) * fraction * (fraction - 2.0) / 2.0,
            (fraction + 1.0) * fraction * (fraction - 1.0) / 6.0,
        ]
    )


def along_lon(column, lon_w, shift_value):
    lon_count = column.shape[-1]
    doubled = jnp.concatenate([column, column], axis=-1)
    result = jnp.zeros_like(column)
    for offset in range(4):
        first = (shift_value + offset - 1) % lon_count
        result = result + lon_w[offset] * lax.dynamic_slice_in_dim(doubled, first, lon_count, 2)
    return result


def per_device(fields, lat_fraction, lon_fraction, lon_shift, departure_row, extents):
    row_count = fields.shape[0]
    band_index = lax.axis_index("lat")
    total_rows = lax.axis_size("lat") * row_count
    first_row = band_index * row_count
    north_bands = []
    south_bands = []
    for distance in range(1, REACH + 1):
        north_bands.insert(0, from_behind(fields, "lat", distance))
        south_bands.append(from_behind(fields, "lat", -distance))
    padded = jnp.concatenate(north_bands + [fields] + south_bands, axis=0)
    low_bound = first_row - extents[0, 0] * row_count + 1
    high_bound = first_row + row_count - 3 + extents[0, 1] * row_count
    departure = jnp.clip(jnp.clip(departure_row, low_bound, high_bound), 1, total_rows - 3)
    local_start = departure - 1 - (first_row - REACH * row_count)

    def one_row(inputs):
        start_value, lat_t, lon_t, shift_value = inputs
        row_block = lax.dynamic_slice_in_dim(padded, start_value, 4, 0)
        lat_w = cubic_weights(lat_t)
        column = (
            lat_w[0] * row_block[0]
            + lat_w[1] * row_block[1]
            + lat_w[2] * row_block[2]
            + lat_w[3] * row_block[3]
        )
        return along_lon(column, cubic_weights(lon_t), shift_value)

    moved = lax.map(one_row, (local_start, lat_fraction, lon_fraction, lon_shift))
    row_ids = first_row + jnp.arange(row_count, dtype=jnp.int32)
    area = jnp.cos(math.pi * (row_ids.astype(jnp.float32) + 0.5) / total_rows - math.pi / 2.0)
    local_before = jnp.sum(area[:, None, None, None] * fields, axis=(0, 2, 3))
    local_after = jnp.sum(area[:, None, None, None] * moved, axis=(0, 2, 3))
    mass_before, mass_after = lax.psum((local_before, local_after), ("lat", "lev"))
    return moved * (mass_before / mass_after)[None, :, None, None]


def solution(mesh):
    return jax.shard_map(
        per_device,
        mesh=mesh,
        in_specs=(
            P("lat", None, "lev", None),
            P("lat"),
            P("lat"),
            P("lat"),
            P("lat"),
            P("lat", None),
        ),
        out_specs=P("lat", None, "lev", None),
        check_vma=False,
    )
```

profile of v0, /device:TPU:0, one launch (start us, length us, event | category | flops | bytes accessed | tf_op | source)
XLA Modules:
  0.0 528.6 jit_solution(7406664660782324728)
XLA Ops:
  0.0 6.4 %collective-permute-start = (f32[10,3,8,2560]{3,2,1,0:T(8,128)}, f32[10,3,8,2560]{3,2,1,0:T(8,128)}, u32[]{:S(2)}, u32[]{:S(2)}) collective-permute-start(f32[10,3,8,2560]{3,2,1,0:T(8,128)} %param.8), channel_id=1, source_target_pairs={{0,8},{2,10},{4,12},{6,14},{8,16},{10,18},{12,20},{14,22},{16,24},... | collective-permute-start | bytes 7372808 | tf_op jit(solution)/shard_map/ppermute | solution.py:14
  6.4 5.8 %collective-permute-start.1 = (f32[10,3,8,2560]{3,2,1,0:T(8,128)}, f32[10,3,8,2560]{3,2,1,0:T(8,128)}, u32[]{:S(2)}, u32[]{:S(2)}) collective-permute-start(f32[10,3,8,2560]{3,2,1,0:T(8,128)} %param.8), channel_id=1, source_target_pairs={{0,6},{2,8},{4,10},{6,12},{8,14},{10,16},{12,18},{14,20},{16,22},{... | collective-permute-start | bytes 7372808 | tf_op jit(solution)/shard_map/ppermute | solution.py:14
  12.2 3.4 collective-permute-start.2
  15.6 2.8 collective-permute-start.3
  23.0 34.9 %collective-permute-done = f32[10,3,8,2560]{3,2,1,0:T(8,128)} collective-permute-done((f32[10,3,8,2560]{3,2,1,0:T(8,128)}, f32[10,3,8,2560]{3,2,1,0:T(8,128)}, u32[]{:S(2)}, u32[]{:S(2)}) %collective-permute-start) | collective-permute-done | bytes 2457632 | tf_op jit(solution)/shard_map/ppermute | solution.py:14
  59.2 1.9 constant_dynamic-update-slice_fusion.8
  61.0 159.4 %collective-permute-done.1 = f32[10,3,8,2560]{3,2,1,0:T(8,128)} collective-permute-done((f32[10,3,8,2560]{3,2,1,0:T(8,128)}, f32[10,3,8,2560]{3,2,1,0:T(8,128)}, u32[]{:S(2)}, u32[]{:S(2)}) %collective-permute-start.1) | collective-permute-done | bytes 2457632 | tf_op jit(solution)/shard_map/ppermute | solution.py:14
  221.7 1.9 constant_dynamic-update-slice_fusion.7
  225.8 1.9 constant_dynamic-update-slice_fusion.6
  227.7 43.9 %collective-permute-done.3 = f32[10,3,8,2560]{3,2,1,0:T(8,128)} collective-permute-done((f32[10,3,8,2560]{3,2,1,0:T(8,128)}, f32[10,3,8,2560]{3,2,1,0:T(8,128)}, u32[]{:S(2)}, u32[]{:S(2)}) %collective-permute-start.3) | collective-permute-done | bytes 2457632 | tf_op jit(solution)/shard_map/ppermute | solution.py:14
  271.6 1.9 constant_dynamic-update-slice_fusion.5
  273.7 1.9 constant_dynamic-update-slice_fusion.3
  276.0 4.1 collective-permute-done.7
  280.3 7.3 %copy-done.1 = f32[90,3,8,2560]{3,2,1,0:T(8,128)} copy-done((f32[90,3,8,2560]{3,2,1,0:T(8,128)}, f32[90,3,8,2560]{3,2,1,0:T(8,128)S(1)}, u32[]{:S(2)}) %copy-start.1) | copy-done | bytes 22118424
  287.6 165.5 %while.15 = (s32[]{:T(128)}, f32[10,3,8,2560]{3,2,1,0:T(8,128)S(1)}, f32[10]{0:T(128)S(1)}, f32[10]{0:T(128)S(1)}, s32[10]{0:T(128)S(1)}, /*index=5*/f32[90,3,8,...) while((s32[]{:T(128)}, ...), condition=%wide.region_1.2_spmd, body=%wide.region_0.1_spmd.sunk | while | flops 1106001 | bytes 1721515 | solution.py:66
  294.6 1.4 fusion.20
  311.1 1.4 fusion.20
  327.7 1.4 fusion.20
  344.2 1.4 fusion.20
  360.8 1.4 fusion.20
  377.3 1.4 fusion.20
  453.1 2.3 multiply_reduce_fusion
  455.4 71.3 %all-reduce = (f32[3]{0:T(128)S(1)}, f32[3]{0:T(128)S(1)}) all-reduce(f32[3]{0:T(128)S(1)} %get-tuple-element.190, f32[3]{0:T(128)S(1)} %get-tuple-element.189), channel_id=1, replica_groups=mesh['lat'=16,'lev'=2] {'lat','lev'}, use_global_device_ids=true, to_apply=%region_3.4 | all-reduce | flops 6 | bytes 48 | tf_op jit(solution)/shard_map/psum | solution.py:71
  526.8 1.8 broadcast_multiply_fusion
  (80 shorter events, 46.7 us)
Async XLA Ops:
  0.0 57.9 %collective-permute-start = (f32[10,3,8,2560]{3,2,1,0:T(8,128)}, f32[10,3,8,2560]{3,2,1,0:T(8,128)}, u32[]{:S(2)}, u32[]{:S(2)}) collective-permute-start(f32[10,3,8,2560]{3,2,1,0:T(8,128)} %param.8), channel_id=1, source_target_pairs={{0,8},{2,10},{4,12},{6,14},{8,16},{10,18},{12,20},{14,22},{16,24},... | collective-permute-start | bytes 7372808 | tf_op jit(solution)/shard_map/ppermute | solution.py:14
  6.4 214.0 %collective-permute-start.1 = (f32[10,3,8,2560]{3,2,1,0:T(8,128)}, f32[10,3,8,2560]{3,2,1,0:T(8,128)}, u32[]{:S(2)}, u32[]{:S(2)}) collective-permute-start(f32[10,3,8,2560]{3,2,1,0:T(8,128)} %param.8), channel_id=1, source_target_pairs={{0,6},{2,8},{4,10},{6,12},{8,14},{10,16},{12,18},{14,20},{16,22},{... | collective-permute-start | bytes 7372808 | tf_op jit(solution)/shard_map/ppermute | solution.py:14
  12.2 212.3 %collective-permute-start.2 = (f32[10,3,8,2560]{3,2,1,0:T(8,128)}, f32[10,3,8,2560]{3,2,1,0:T(8,128)}, u32[]{:S(2)}, u32[]{:S(2)}) collective-permute-start(f32[10,3,8,2560]{3,2,1,0:T(8,128)} %param.8), channel_id=1, source_target_pairs={{0,4},{2,6},{4,8},{6,10},{8,12},{10,14},{12,16},{14,18},{16,20},{1... | collective-permute-start | bytes 7372808 | tf_op jit(solution)/shard_map/ppermute | solution.py:14
  15.6 256.0 %collective-permute-start.3 = (f32[10,3,8,2560]{3,2,1,0:T(8,128)}, f32[10,3,8,2560]{3,2,1,0:T(8,128)}, u32[]{:S(2)}, u32[]{:S(2)}) collective-permute-start(f32[10,3,8,2560]{3,2,1,0:T(8,128)} %param.8), channel_id=1, source_target_pairs={{0,2},{2,4},{4,6},{6,8},{8,10},{10,12},{12,14},{14,16},{16,18},{18... | collective-permute-start | bytes 7372808 | tf_op jit(solution)/shard_map/ppermute | solution.py:14
  18.4 255.3 %collective-permute-start.4 = (f32[10,3,8,2560]{3,2,1,0:T(8,128)}, f32[10,3,8,2560]{3,2,1,0:T(8,128)}, u32[]{:S(2)}, u32[]{:S(2)}) collective-permute-start(f32[10,3,8,2560]{3,2,1,0:T(8,128)} %param.8), channel_id=1, source_target_pairs={{2,0},{4,2},{6,4},{8,6},{10,8},{12,10},{14,12},{16,14},{18,16},{20... | collective-permute-start | bytes 7372808 | tf_op jit(solution)/shard_map/ppermute | solution.py:14
  23.0 197.4 %copy-start = (f32[10,3,8,2560]{3,2,1,0:T(8,128)S(1)}, f32[10,3,8,2560]{3,2,1,0:T(8,128)}, u32[]{:S(2)}) copy-start(f32[10,3,8,2560]{3,2,1,0:T(8,128)} %param.8) | copy-start | bytes 7372804
  57.9 217.7 %collective-permute-start.5 = (f32[10,3,8,2560]{3,2,1,0:T(8,128)}, f32[10,3,8,2560]{3,2,1,0:T(8,128)S(1)}, u32[]{:S(2)}, u32[]{:S(2)}) collective-permute-start(f32[10,3,8,2560]{3,2,1,0:T(8,128)} %param.8), channel_id=1, source_target_pairs={{4,0},{6,2},{8,4},{10,6},{12,8},{14,10},{16,12},{18,14},{20,16},{2... | collective-permute-start | bytes 7372808 | tf_op jit(solution)/shard_map/ppermute | solution.py:14
  220.4 55.4 %collective-permute-start.6 = (f32[10,3,8,2560]{3,2,1,0:T(8,128)S(1)}, f32[10,3,8,2560]{3,2,1,0:T(8,128)S(1)}, u32[]{:S(2)}, u32[]{:S(2)}) collective-permute-start(f32[10,3,8,2560]{3,2,1,0:T(8,128)S(1)} %copy-done), channel_id=1, source_target_pairs={{6,0},{8,2},{10,4},{12,6},{14,8},{16,10},{18,12},{20,14},{22,16},{... | collective-permute-start | bytes 7372808 | tf_op jit(solution)/shard_map/ppermute | solution.py:14
  224.5 55.6 %collective-permute-start.7 = (f32[10,3,8,2560]{3,2,1,0:T(8,128)S(1)}, f32[10,3,8,2560]{3,2,1,0:T(8,128)S(1)}, u32[]{:S(2)}, u32[]{:S(2)}) collective-permute-start(f32[10,3,8,2560]{3,2,1,0:T(8,128)S(1)} %copy-done), channel_id=1, source_target_pairs={{8,0},{10,2},{12,4},{14,6},{16,8},{18,10},{20,12},{22,14},{24,16},... | collective-permute-start | bytes 7372808 | tf_op jit(solution)/shard_map/ppermute | solution.py:14
  276.0 11.7 %copy-start.2 = (f32[10]{0:T(128)S(1)}, f32[10]{0:T(128)}, u32[]{:S(2)}) copy-start(f32[10]{0:T(128)} %param.10) | copy-start | bytes 124
  276.0 11.7 %copy-start.3 = (f32[10]{0:T(128)S(1)}, f32[10]{0:T(128)}, u32[]{:S(2)}) copy-start(f32[10]{0:T(128)} %param.9) | copy-start | bytes 124
  276.0 11.6 %copy-start.4 = (s32[10]{0:T(128)S(1)}, s32[10]{0:T(128)}, u32[]{:S(2)}) copy-start(s32[10]{0:T(128)} %param.11) | copy-start | bytes 124
  280.3 7.3 %copy-start.1 = (f32[90,3,8,2560]{3,2,1,0:T(8,128)}, f32[90,3,8,2560]{3,2,1,0:T(8,128)S(1)}, u32[]{:S(2)}) copy-start(f32[90,3,8,2560]{3,2,1,0:T(8,128)S(1)} %constant_dynamic-update-slice_fusion) | copy-start | bytes 66355204
where the time goes:
time: 531 us; the launch traced here: 529 us
  waiting for transfers between devices  243 us (46%)
  loops' own time  119 us (22%)
  blocking collectives  71.3 us (13%)
  local copies, waits for them, and re-layouts  44.8 us (8%)
  other arithmetic  24.8 us (5%)
  starting transfers between devices  23.5 us (4%)
    ppermute x8, waiting for transfers between devices, from_behind(): return lax.ppermute(block, axis, route)  243 us
    another operation x1, loops' own time, per_device(): lax.map(one_row, (local_start, lat_fraction, lon_fraction, lon_shift))  119 us
    psum x1, blocking collectives, per_device(): lax.psum((local_before, local_after), ('lat', 'lev'))  71.3 us
    dynamic_slice x40, local copies, waits for them, and re-layouts, per_device(): lax.map(one_row, (local_start, lat_fraction, lon_fraction, lon_shift))  26.1 us
    ppermute x8, starting transfers between devices, from_behind(): return lax.ppermute(block, axis, route)  23.5 us
    unnamed x18, local copies, waits for them, and re-layouts  17.2 us
    add x10, other arithmetic, one_row(): lat_w[0] * row_block[0] + lat_w[1] * row_block[1] + lat_w[2] * row_block[2]  13.8 us
  transfers between devices with their start and end apart: 8, of which 5 were waited for; matrix products, arithmetic and copies ran while one was open for 2% of the time, Pallas kernels for 0%

commit v1 on v0

v1 whole, which is shorter than its diff:
```python
import functools
import math

import jax
import jax.numpy as jnp
from jax import lax
from jax.experimental import pallas as pl
from jax.experimental.pallas import tpu as pltpu
from jax.sharding import PartitionSpec as P

REACH = 4
LANES = 128
DEPTH = 3
MESH = pl.DeviceIdType.MESH

UP = {
    0: [],
    1: [(0, 1), (0, 2), (0, 0)],
    2: [(0, 0), (0, 1), (0, 2), (1, 0)],
    3: [(1, 1), (1, 2), (1, 0), (0, 0)],
}
UP_OVER_ONE = {3: [(2, 0), (2, 1), (2, 2)], 2: [(1, 1), (1, 2)]}
UP_OVER_TWO = {3: [(0, 1), (0, 2)]}


def arrivals(member):
    def both(table):
        up = [(1, m, h) for m, h in table.get(member, [])]
        down = [(-1, 3 - m, h) for m, h in table.get(3 - member, [])]
        return up + down

    one = [(0, member ^ 1, h) for h in range(3)] + [(0, member ^ 3, 0)] + both(UP_OVER_ONE)
    two = [(0, member ^ 2, h) for h in range(3)] + [(0, member ^ 3, h) for h in (1, 2)] + both(UP_OVER_TWO)
    up = [(1, member, h) for h in range(3)] + [(1, m, h) for m, h in UP[member]]
    down = [(-1, member, h) for h in range(3)] + [(-1, 3 - m, h) for m, h in UP[3 - member]]
    return {"one": one, "two": two, "up": up, "down": down}


LINKS = ("one", "two", "up", "down")


def exchange_kernel(bands, fields_ref, halo_ref, send_sem, recv_sem):
    band = lax.axis_index("lat")
    group, position = band // 4, lax.rem(band, 4)
    has_up = group < bands // 4 - 1
    has_down = group > 0
    rows, field_count = fields_ref.shape[:2]

    def cut(part):
        first = field_count * part // 3
        return pl.ds(first, field_count * (part + 1) // 3 - first)

    def slot_of(distance):
        return distance + 4 if distance < 0 else distance + 3

    def halo_part(distance, part):
        return halo_ref.at[pl.ds(slot_of(distance) * rows, rows), cut(part)]

    def when(offset, body):
        if offset == 0:
            body()
        else:
            pl.when(has_up if offset == 1 else has_down)(body)

    barrier = pltpu.get_barrier_semaphore()

    def greet(step, condition):
        def body():
            pl.semaphore_signal(barrier, inc=1, device_id={"lat": band + step}, device_id_type=MESH)

        pl.when(condition)(body)

    even, low = lax.rem(position, 2) == 0, position < 2
    greet(1, even)
    greet(-1, jnp.logical_not(even))
    greet(2, low)
    greet(-2, jnp.logical_not(low))
    greet(4, has_up)
    greet(-4, has_down)
    pl.semaphore_wait(barrier, 2 + has_up.astype(jnp.int32) + has_down.astype(jnp.int32))

    for member in range(4):

        def run(member=member):
            incoming = arrivals(member)
            came_over = {item: (link, k) for link in LINKS for k, item in enumerate(incoming[link])}
            waited = set()

            def wait_for(item):
                if item in waited:
                    return
                waited.add(item)
                offset, m, h = item
                link, k = came_over[item]
                place = halo_part(4 * offset + m - member, h)

                def body():
                    pltpu.make_async_remote_copy(
                        src_ref=place, dst_ref=place,
                        send_sem=send_sem.at[LINKS.index(link), k],
                        recv_sem=recv_sem.at[LINKS.index(link), k],
                        device_id={"lat": band}, device_id_type=MESH,
                    ).wait_recv()

                when(offset, body)

            targets = [
                ("up", member, -4, -1),
                ("down", member, 4, 1),
                ("one", member ^ 1, (member ^ 1) - member, 0),
                ("two", member ^ 2, (member ^ 2) - member, 0),
            ]
            lists = [arrivals(target)[link] for link, target, _, _ in targets]
            sends = []
            for k in range(max(len(one) for one in lists)):
                for (link, target, step, group_step), items in zip(targets, lists):
                    if k >= len(items):
                        continue
                    offset, m, h = items[k]
                    here = offset + group_step
                    mine = here == 0 and m == member
                    if not mine:
                        wait_for((here, m, h))
                    source = fields_ref.at[:, cut(h)] if mine else halo_part(4 * here + m - member, h)
                    copy = pltpu.make_async_remote_copy(
                        src_ref=source,
                        dst_ref=halo_part(4 * offset + m - target, h),
                        send_sem=send_sem.at[LINKS.index(link), k],
                        recv_sem=recv_sem.at[LINKS.index(link), k],
                        device_id={"lat": band + step}, device_id_type=MESH,
                    )
                    condition = group_step if group_step else here
                    when(condition, copy.start)
                    sends.append((condition, copy))
            for k in range(max(len(incoming[link]) for link in LINKS)):
                for link in LINKS:
                    if k < len(incoming[link]):
                        wait_for(incoming[link][k])
            for condition, copy in sends:
                when(condition, copy.wait_send)

        pl.when(position == member)(run)


def exchange(fields):
    bands = lax.axis_size("lat")
    rows = fields.shape[0]
    if bands % 4 or fields.shape[1] < 3:
        blocks = []
        for distance in list(range(-REACH, 0)) + list(range(1, REACH + 1)):
            route = [(i + distance, i) for i in range(bands) if 0 <= i + distance < bands]
            blocks.append(lax.ppermute(fields, "lat", route))
        return jnp.concatenate(blocks, axis=0)
    return pl.pallas_call(
        functools.partial(exchange_kernel, bands),
        out_shape=jax.ShapeDtypeStruct((2 * REACH * rows,) + fields.shape[1:], fields.dtype),
        in_specs=[pl.BlockSpec(memory_space=pl.ANY)],
        out_specs=pl.BlockSpec(memory_space=pl.ANY),
        scratch_shapes=[pltpu.SemaphoreType.DMA((4, 7)), pltpu.SemaphoreType.DMA((4, 7))],
        compiler_params=pltpu.CompilerParams(collective_id=0, has_side_effects=True),
        cost_estimate=pl.CostEstimate(flops=0, bytes_accessed=16 * fields.size * 4 * 10, transcendentals=0),
        name="exchange",
    )(fields)


def row_kernel(start_ref, shift_ref, lat_w_ref, lon_w_ref, table_ref, area_ref, fields_ref, halo_ref, out_ref,
               held, doubled, ratio, sem):
    row = pl.program_id(0)
    row_count = pl.num_programs(0)
    rows, field_count, _, lon_count = fields_ref.shape
    tiles = lon_count // LANES

    def fetch(index):
        slot = lax.rem(index, DEPTH)
        for a in range(4):
            place = start_ref[index] + a
            own = jnp.logical_and(place >= REACH * rows, place < (REACH + 1) * rows)
            target = held.at[slot, a]

            @pl.when(own)
            def _():
                pltpu.make_async_copy(fields_ref.at[place - REACH * rows], target, sem.at[slot, a]).start()

            @pl.when(jnp.logical_not(own))
            def _():
                away = jnp.where(place < REACH * rows, place, place - rows)
                pltpu.make_async_copy(halo_ref.at[away], target, sem.at[slot, a]).start()

    @pl.when(row == 0)
    def _():
        for index in range(min(DEPTH - 1, rows)):
            fetch(index)
        weight = table_ref[field_count:field_count + 1, :]
        for f in range(field_count):
            total = table_ref[f:f + 1, :]
            before = jnp.sum(total * area_ref[...], axis=1, keepdims=True)
            after = jnp.sum(total * weight, axis=1, keepdims=True)
            ratio[f] = jnp.broadcast_to(before / after, ratio.shape[1:])

    @pl.when(row + DEPTH - 1 < row_count)
    def _():
        fetch(row + DEPTH - 1)

    slot = lax.rem(row, DEPTH)
    for a in range(4):
        pltpu.make_async_copy(fields_ref.at[0], held.at[slot, a], sem.at[slot, a]).wait()
    lane = lax.broadcasted_iota(jnp.int32, (out_ref.shape[2], LANES), 1)
    for f in range(field_count):
        column = lat_w_ref[row, 0] * held[slot, 0, f]
        for a in range(1, 4):
            column = column + lat_w_ref[row, a] * held[slot, a, f]
        doubled[f, :, 0:lon_count] = column
        doubled[f, :, lon_count:2 * lon_count] = column
        sums = [None] * tiles
        for k in range(4):
            first = lax.rem(shift_ref[row] + k - 1 + lon_count, lon_count)
            whole, rest = first // LANES, lax.rem(first, LANES)
            turn = lax.rem(LANES - rest, LANES)
            keep = lane < LANES - rest
            weight = lon_w_ref[row, k] * ratio[f]
            turned = []
            for t in range(tiles + 1):
                at = pl.multiple_of((whole + t) * LANES, LANES)
                turned.append(pltpu.roll(doubled[f, :, pl.ds(at, LANES)], turn, 1))
            for t in range(tiles):
                term = weight * jnp.where(keep, turned[t], turned[t + 1])
                sums[t] = term if sums[t] is None else sums[t] + term
        for t in range(tiles):
            out_ref[0, f, :, t * LANES:(t + 1) * LANES] = sums[t]


def rows_of(start, shift, lat_w, lon_w, table, area, fields, halo):
    rows, field_count, levels, lon_count = fields.shape
    smem = pl.BlockSpec(memory_space=pltpu.SMEM)
    return pl.pallas_call(
        row_kernel,
        grid=(rows,),
        out_shape=jax.ShapeDtypeStruct(fields.shape, fields.dtype),
        in_specs=[smem] * 4 + [pl.BlockSpec(memory_space=pltpu.VMEM)] * 2 + [pl.BlockSpec(memory_space=pl.ANY)] * 2,
        out_specs=pl.BlockSpec((1, field_count, levels, lon_count), lambda r: (r, 0, 0, 0)),
        scratch_shapes=[
            pltpu.VMEM((DEPTH, 4, field_count, levels, lon_count), jnp.float32),
            pltpu.VMEM((field_count, levels, 2 * lon_count), jnp.float32),
            pltpu.VMEM((field_count, levels, LANES), jnp.float32),
            pltpu.SemaphoreType.DMA((DEPTH, 4)),
        ],
        compiler_params=pltpu.CompilerParams(dimension_semantics=("arbitrary",)),
        name="rows",
    )(start, shift, lat_w, lon_w, table, area, fields, halo)


def cubic_weights(fraction):
    return jnp.stack(
        [
            -fraction * (fraction - 1.0) * (fraction - 2.0) / 6.0,
            (fraction + 1.0) * (fraction - 1.0) * (fraction - 2.0) / 2.0,
            -(fraction + 1.0) * fraction * (fraction - 2.0) / 2.0,
            (fraction + 1.0) * fraction * (fraction - 1.0) / 6.0,
        ],
        axis=-1,
    )


def area_of(row_ids, total_rows):
    return jnp.cos(math.pi * (row_ids.astype(jnp.float32) + 0.5) / total_rows - math.pi / 2.0)


def per_device(fields, lat_fraction, lon_fraction, lon_shift, departure_row, extents):
    rows = fields.shape[0]
    total_rows = lax.axis_size("lat") * rows
    first_row = lax.axis_index("lat") * rows
    low_bound = first_row - extents[0, 0] * rows + 1
    high_bound = first_row + rows - 3 + extents[0, 1] * rows
    departure = jnp.clip(jnp.clip(departure_row, low_bound, high_bound), 1, total_rows - 3)
    start = departure - 1 - (first_row - REACH * rows)
    lat_w, lon_w = cubic_weights(lat_fraction), cubic_weights(lon_fraction)

    row_area = area_of(first_row + jnp.arange(rows, dtype=jnp.int32), total_rows)
    share = (row_area * jnp.sum(lon_w, axis=1))[:, None] * lat_w / lax.axis_size("lev")
    all_rows = jnp.arange(total_rows, dtype=jnp.int32)
    reads = (departure - 1)[:, None] + jnp.arange(4, dtype=jnp.int32)[None, :]
    taken = jnp.sum(jnp.where(reads[:, :, None] == all_rows, share[:, :, None], 0.0), axis=(0, 1))
    sums = jnp.sum(fields, axis=(2, 3))
    mine = (first_row + jnp.arange(rows, dtype=jnp.int32))[:, None, None] == all_rows
    placed = jnp.sum(jnp.where(mine, sums[:, :, None], 0.0), axis=0)
    table = lax.psum(jnp.concatenate([placed, taken[None, :]], axis=0), ("lat", "lev"))

    halo = exchange(fields)
    return rows_of(start, lon_shift, lat_w, lon_w, table, area_of(all_rows, total_rows)[None, :], fields, halo)


def solution(mesh):
    return jax.shard_map(
        per_device,
        mesh=mesh,
        in_specs=(
            P("lat", None, "lev", None),
            P("lat"),
            P("lat"),
            P("lat"),
            P("lat"),
            P("lat", None),
        ),
        out_specs=P("lat", None, "lev", None),
        check_vma=False,
    )
```

time: 531 us -> 186 us (0.35)
  waiting for transfers between devices: 243 us -> 0 us
  Pallas kernels: 0 us -> 134 us
  loops' own time: 119 us -> 0 us
  local copies, waits for them, and re-layouts: 44.8 us -> 2.78 us
  blocking collectives: 71.3 us -> 42 us
  starting transfers between devices: 23.5 us -> 0 us
  other arithmetic: 24.8 us -> 5.41 us
    ppermute x8 -> x0, waiting for transfers between devices: 243 us -> none  [from_behind(): return lax.ppermute(block, axis, route)]
    pallas_call x0 -> x2, Pallas kernels: none -> 134 us  [the longest x1 125 us: exchange(): pl.pallas_call(functools.partial(exchange_kernel, bands), out_shape=jax.S...]
    another operation x1 -> x0, loops' own time: 119 us -> none  [per_device(): lax.map(one_row, (local_start, lat_fraction, lon_fraction, lon_shift))]
    psum x1, blocking collectives: 71.3 us -> 42 us  [per_device(): lax.psum(jnp.concatenate([placed, taken[None, :]], axis=0), ('lat', 'lev'))]
    dynamic_slice x40 -> x0, local copies, waits for them, and re-layouts: 26.1 us -> none  [per_device(): lax.map(one_row, (local_start, lat_fraction, lon_fraction, lon_shift))]
    ppermute x8 -> x0, starting transfers between devices: 23.5 us -> none  [from_behind(): return lax.ppermute(block, axis, route)]
    unnamed x18 -> x0, local copies, waits for them, and re-layouts: 17.2 us -> none
    add x10 -> x2, other arithmetic: 13.8 us -> 0.07 us  [the longest x1 0.07 us: per_device(): reads = (departure - 1)[:, None] + jnp.arange(4, dtype=jnp.int32)[None, :]]
  transfers between devices with their start and end apart: 8 -> 0, of which waited for: 5 -> 0; matrix products, arithmetic and copies ran while one was open for 2% -> 0% of each run, Pallas kernels for 0% -> 0%
where the time goes in v1:
time: 186 us; the launch traced here: 185 us
  Pallas kernels  134 us (72%)
  blocking collectives  42 us (23%)
  other arithmetic  5.41 us (3%)
  local copies, waits for them, and re-layouts  2.78 us (1%)
    pallas_call x1, Pallas kernels, exchange(): pl.pallas_call(functools.partial(exchange_kernel, bands), out_shape=jax.S...  125 us
    psum x1, blocking collectives, per_device(): lax.psum(jnp.concatenate([placed, taken[None, :]], axis=0), ('lat', 'lev'))  42 us
    pallas_call x1, Pallas kernels, rows_of(): pl.pallas_call(row_kernel, grid=(rows,), out_shape=jax.ShapeDtypeStruct(f...  9.02 us

profile of v1, /device:TPU:0, one launch (start us, length us, event | category | flops | bytes accessed | tf_op | source)
XLA Modules:
  0.0 185.2 jit_solution(5534928262194917909)
XLA Ops:
  0.0 0.6 add_cosine_fusion.area_ref
  0.6 1.3 fusion.4
  3.3 1.1 broadcast_subtract_fusion
  4.4 0.7 add_multiply_fusion
  5.2 0.7 multiply_bitcast_fusion.3
  5.8 0.1 iota_compare_fusion.1
  5.9 0.1 copy.18
  6.0 0.7 copy.20.lon_w_ref
  6.7 0.7 copy.19.lat_w_ref
  7.4 0.1 iota_add_fusion
  7.4 0.1 select_reduce_fusion
  7.6 1.9 %reduce_sum.43 = f32[10,3]{1,0:T(8,128)S(1)} reduce(f32[10,3,8,2560]{3,2,1,0:T(8,128)} %fields_ref.3, f32[]{:T(128)} %constant.62.clone.1), dimensions={2,3}, to_apply=%region_0.1 | reduce | flops 614370 | bytes 2457724 | tf_op jit(solution)/shard_map/reduce_sum | solution.py:283
  9.5 0.1 select_reduce_fusion.1
  9.6 42.0 %psum.7.table_ref = f32[4,160]{1,0:T(4,128)} all-reduce(f32[4,160]{1,0:T(4,128)S(1)} %pad_maximum_fusion), channel_id=1, replica_groups=mesh['lat'=16,'lev'=2] {'lat','lev'}, use_global_device_ids=true, to_apply=%region_3.4 | all-reduce | flops 640 | bytes 5120 | tf_op jit(solution)/shard_map/psum | solution.py:286
  51.6 124.6 %exchange.1.halo_ref = f32[80,3,8,2560]{3,2,1,0:T(8,128)} custom-call(f32[10,3,8,2560]{3,2,1,0:T(8,128)} %fields_ref.3), custom_call_target="tpu_custom_call" | custom-call | bytes 393216000 | tf_op jit(solution)/shard_map/exchange/pallas_call | solution.py:154
  176.2 9.0 %rows.1 = f32[10,3,8,2560]{3,2,1,0:T(8,128)} custom-call(s32[10]{0:T(128)} %get-tuple-element.5.start_ref, s32[10]{0:T(128)} %shift_ref.1, f32[10,4]{1,0:T(8,128)} %copy.19.lat_w_ref, f32[10,4]{1,0:T(8,128)} %copy.20.lon_w_ref, f32[4,160]{1,0:T(4,128)} %psum.7.table_ref, f32[1,160]{1,0:T(1,128)} %add_cosine_fusion.area_ref, f32[10,3,8,2560]{3,2,1,0:T(8,128)} %fields_ref.3, ...), custom_call_target="tpu_custom_call" | custom-call | tf_op jit(solution)/shard_map/rows/pallas_call | solution.py:235
  (4 shorter events, 0.0 us)

commit v2 on v1

v2 whole, which is shorter than its diff:
```python
import functools
import math

import jax
import jax.numpy as jnp
import numpy as np
from jax import lax
from jax.experimental import pallas as pl
from jax.experimental.pallas import tpu as pltpu
from jax.sharding import PartitionSpec as P

REACH = 4
LANES = 128
DEPTH = 3
MESH = pl.DeviceIdType.MESH

UP = {
    0: [],
    1: [(0, 1), (0, 2), (0, 0)],
    2: [(0, 0), (0, 1), (0, 2), (1, 0)],
    3: [(1, 1), (1, 2), (1, 0), (0, 0)],
}
UP_OVER_ONE = {3: [(2, 0), (2, 1), (2, 2)], 2: [(1, 1), (1, 2)]}
UP_OVER_TWO = {3: [(0, 1), (0, 2)]}


def arrivals(member):
    def both(table):
        up = [(1, m, h) for m, h in table.get(member, [])]
        down = [(-1, 3 - m, h) for m, h in table.get(3 - member, [])]
        return up + down

    one = [(0, member ^ 1, h) for h in range(3)] + [(0, member ^ 3, 0)] + both(UP_OVER_ONE)
    two = [(0, member ^ 2, h) for h in range(3)] + [(0, member ^ 3, h) for h in (1, 2)] + both(UP_OVER_TWO)
    up = [(1, member, h) for h in range(3)] + [(1, m, h) for m, h in UP[member]]
    down = [(-1, member, h) for h in range(3)] + [(-1, 3 - m, h) for m, h in UP[3 - member]]
    return {"one": one, "two": two, "up": up, "down": down}


LINKS = ("one", "two", "up", "down")


def cubic(t):
    sixth = 1.0 / 6.0
    return (
        -t * (t - 1.0) * (t - 2.0) * sixth,
        (t + 1.0) * (t - 1.0) * (t - 2.0) * 0.5,
        -(t + 1.0) * t * (t - 2.0) * 0.5,
        (t + 1.0) * t * (t - 1.0) * sixth,
    )


def departure_of(row, first_row, rows, total_rows, departure_ref, extents_ref):
    low = first_row - extents_ref[0, 0] * rows + 1
    high = first_row + rows - 3 + extents_ref[0, 1] * rows
    inside = jnp.minimum(jnp.maximum(departure_ref[row], low), high)
    return jnp.minimum(jnp.maximum(inside, 1), total_rows - 3)


def exchange_kernel(bands, levs, lat_t_ref, lon_t_ref, departure_ref, extents_ref, area_ref, fields_ref,
                    halo_ref, table_ref, held, mine, met, sent, gathered, send_sem, recv_sem, local_sem,
                    table_send_sem, table_recv_sem):
    band, lev = lax.axis_index("lat"), lax.axis_index("lev")
    group, position = band // 4, lax.rem(band, 4)
    groups = bands // 4
    has_up = group < groups - 1
    has_down = group > 0
    rows, field_count = fields_ref.shape[:2]
    first_row, total_rows = band * rows, bands * rows
    step_one = 1 - 2 * lax.rem(position, 2)
    step_two = 2 - 4 * (position // 2)
    across = [{"lev": 1 - lev}, {"lat": band + step_one}, {"lat": band + step_two}]
    others = [{"lat": lax.rem(band + 4 * j, bands)} for j in range(1, groups)]

    barrier = pltpu.get_barrier_semaphore()
    for peer in across + others:
        pl.semaphore_signal(barrier, inc=1, device_id=peer, device_id_type=MESH)
    pl.semaphore_wait(barrier, len(across) + len(others))

    def cut(part):
        first = field_count * part // 3
        return pl.ds(first, field_count * (part + 1) // 3 - first)

    def halo_part(distance, part):
        slot = distance + 4 if distance < 0 else distance + 3
        return halo_ref.at[pl.ds(slot * rows, rows), cut(part)]

    def when(offset, body):
        if offset == 0:
            body()
        else:
            pl.when(has_up if offset == 1 else has_down)(body)

    came_over = [
        {item: (link, k) for link, items in arrivals(member).items() for k, item in enumerate(items)}
        for member in range(4)
    ]
    waited = [set() for _ in range(4)]

    def wait_for(member, item):
        if item in waited[member]:
            return
        waited[member].add(item)
        offset, m, h = item
        link, k = came_over[member][item]
        place = halo_part(4 * offset + m - member, h)
        when(
            offset,
            lambda: pltpu.make_async_remote_copy(
                src_ref=place, dst_ref=place,
                send_sem=send_sem.at[LINKS.index(link), k],
                recv_sem=recv_sem.at[LINKS.index(link), k],
                device_id={"lat": band}, device_id_type=MESH,
            ).wait_recv(),
        )

    def targets(member):
        return [
            ("up", member, -4, -1),
            ("down", member, 4, 1),
            ("one", member ^ 1, (member ^ 1) - member, 0),
            ("two", member ^ 2, (member ^ 2) - member, 0),
        ]

    def sends(member, k):
        for link, target, step, group_step in targets(member):
            items = arrivals(target)[link]
            if k < len(items):
                offset, m, h = items[k]
                here = offset + group_step
                own = here == 0 and m == member
                copy = pltpu.make_async_remote_copy(
                    src_ref=fields_ref.at[:, cut(h)] if own else halo_part(4 * here + m - member, h),
                    dst_ref=halo_part(4 * offset + m - target, h),
                    send_sem=send_sem.at[LINKS.index(link), k],
                    recv_sem=recv_sem.at[LINKS.index(link), k],
                    device_id={"lat": band + step}, device_id_type=MESH,
                )
                yield (None if own else (here, m, h)), (group_step if group_step else here), copy

    def on_each(body):
        for member in range(4):
            pl.when(position == member)(functools.partial(body, member))

    def send_pieces(*steps):
        def body(member):
            for k in steps:
                for item, condition, copy in sends(member, k):
                    if item is not None:
                        wait_for(member, item)
                    when(condition, copy.start)

        on_each(body)

    def table_copy(n, source, target, peer):
        return pltpu.make_async_remote_copy(
            src_ref=source, dst_ref=target, send_sem=table_send_sem.at[n], recv_sem=table_recv_sem.at[n],
            device_id=peer, device_id_type=MESH,
        )

    load = pltpu.make_async_copy(fields_ref, held, local_sem)
    load.start()
    send_pieces(0)

    lane = lax.broadcasted_iota(jnp.int32, (1, table_ref.shape[1]), 1)
    taken = jnp.zeros(lane.shape, jnp.float32)
    for row in range(rows):
        departure = departure_of(row, first_row, rows, total_rows, departure_ref, extents_ref)
        lon_w = cubic(lon_t_ref[row])
        share = area_ref[first_row + row] * (lon_w[0] + lon_w[1] + lon_w[2] + lon_w[3]) * (1.0 / levs)
        for a, weight in enumerate(cubic(lat_t_ref[row])):
            taken = taken + jnp.where(lane == departure - 1 + a, share * weight, 0.0)
    load.wait()
    sums = [jnp.zeros(lane.shape, jnp.float32) for _ in range(field_count)]
    for row in range(rows):
        for f in range(field_count):
            total = jnp.sum(jnp.sum(held[row, f], axis=0, keepdims=True), axis=1, keepdims=True)
            sums[f] = sums[f] + jnp.where(lane == first_row + row, total, 0.0)
    mine[...] = jnp.zeros_like(mine)
    for f in range(field_count):
        mine[f:f + 1, :] = sums[f]
    mine[field_count:field_count + 1, :] = taken

    def table_step(n):
        return table_copy(n, mine if n == 0 else sent.at[n - 1], met.at[n], across[n])

    def table_add(n):
        table_step(n).wait_recv()
        sent[n] = (mine[...] if n == 0 else sent[n - 1]) + met[n]

    table_step(0).start()
    table_add(0)
    table_step(1).start()
    send_pieces(1, 2)
    table_add(1)
    table_step(2).start()
    send_pieces(3, 4)
    table_add(2)
    last = [table_copy(3 + j, sent.at[2], gathered.at[j], peer) for j, peer in enumerate(others)]
    for copy in last:
        copy.start()
    send_pieces(5, 6)
    for copy in last:
        copy.wait_recv()
    result = sent[2]
    for j in range(len(others)):
        result = result + gathered[j]
    table_ref[...] = result

    def finish(member):
        for k in range(7):
            for link in LINKS:
                items = arrivals(member)[link]
                if k < len(items):
                    wait_for(member, items[k])
        for k in range(7):
            for _, condition, copy in sends(member, k):
                when(condition, copy.wait_send)

    on_each(finish)
    for n in range(3):
        table_step(n).wait_send()
    for copy in last:
        copy.wait_send()


def exchange(lat_t, lon_t, departure_row, extents, area, fields):
    bands, levs = lax.axis_size("lat"), lax.axis_size("lev")
    rows, field_count = fields.shape[:2]
    table = ((field_count + 8) // 8 * 8, -(-bands * rows // LANES) * LANES)
    others = bands // 4 - 1
    return pl.pallas_call(
        functools.partial(exchange_kernel, bands, levs),
        out_shape=(
            jax.ShapeDtypeStruct((2 * REACH * rows,) + fields.shape[1:], fields.dtype),
            jax.ShapeDtypeStruct(table, jnp.float32),
        ),
        in_specs=[pl.BlockSpec(memory_space=pltpu.SMEM)] * 5 + [pl.BlockSpec(memory_space=pl.ANY)],
        out_specs=(pl.BlockSpec(memory_space=pl.ANY), pl.BlockSpec(memory_space=pltpu.VMEM)),
        scratch_shapes=[
            pltpu.VMEM(fields.shape, jnp.float32),
            pltpu.VMEM(table, jnp.float32),
            pltpu.VMEM((3,) + table, jnp.float32),
            pltpu.VMEM((3,) + table, jnp.float32),
            pltpu.VMEM((max(others, 1),) + table, jnp.float32),
            pltpu.SemaphoreType.DMA((4, 7)),
            pltpu.SemaphoreType.DMA((4, 7)),
            pltpu.SemaphoreType.DMA,
            pltpu.SemaphoreType.DMA((3 + others,)),
            pltpu.SemaphoreType.DMA((3 + others,)),
        ],
        compiler_params=pltpu.CompilerParams(collective_id=0, has_side_effects=True),
        name="exchange",
    )(lat_t, lon_t, departure_row, extents, area, fields)


def row_kernel(bands, lat_t_ref, lon_t_ref, shift_ref, departure_ref, extents_ref, table_ref, area_ref, fields_ref,
               halo_ref, out_ref, held, doubled, ratio, sem):
    row = pl.program_id(0)
    row_count = pl.num_programs(0)
    rows, field_count, _, lon_count = fields_ref.shape
    tiles = lon_count // LANES
    first_row = lax.axis_index("lat") * rows

    def fetch(index):
        slot = lax.rem(index, DEPTH)
        departure = departure_of(index, first_row, rows, bands * rows, departure_ref, extents_ref)
        start = departure - 1 - (first_row - REACH * rows)
        for a in range(4):
            place = start + a
            own = jnp.logical_and(place >= REACH * rows, place < (REACH + 1) * rows)
            target = held.at[slot, a]

            @pl.when(own)
            def _():
                pltpu.make_async_copy(fields_ref.at[place - REACH * rows], target, sem.at[slot, a]).start()

            @pl.when(jnp.logical_not(own))
            def _():
                away = jnp.where(place < REACH * rows, place, place - rows)
                pltpu.make_async_copy(halo_ref.at[away], target, sem.at[slot, a]).start()

    @pl.when(row == 0)
    def _():
        for index in range(min(DEPTH - 1, rows)):
            fetch(index)
        weight = table_ref[field_count:field_count + 1, :]
        for f in range(field_count):
            total = table_ref[f:f + 1, :]
            before = jnp.sum(total * area_ref[...], axis=1, keepdims=True)
            after = jnp.sum(total * weight, axis=1, keepdims=True)
            ratio[f] = jnp.broadcast_to(before / after, ratio.shape[1:])

    @pl.when(row + DEPTH - 1 < row_count)
    def _():
        fetch(row + DEPTH - 1)

    slot = lax.rem(row, DEPTH)
    for a in range(4):
        pltpu.make_async_copy(fields_ref.at[0], held.at[slot, a], sem.at[slot, a]).wait()
    lat_w, lon_w = cubic(lat_t_ref[row]), cubic(lon_t_ref[row])
    lane = lax.broadcasted_iota(jnp.int32, (out_ref.shape[2], LANES), 1)
    for f in range(field_count):
        column = lat_w[0] * held[slot, 0, f]
        for a in range(1, 4):
            column = column + lat_w[a] * held[slot, a, f]
        doubled[f, :, 0:lon_count] = column
        doubled[f, :, lon_count:2 * lon_count] = column
        sums = [None] * tiles
        for k in range(4):
            first = lax.rem(shift_ref[row] + k - 1 + lon_count, lon_count)
            whole, rest = first // LANES, lax.rem(first, LANES)
            turn = lax.rem(LANES - rest, LANES)
            keep = lane < LANES - rest
            weight = lon_w[k] * ratio[f]
            turned = []
            for t in range(tiles + 1):
                at = pl.multiple_of((whole + t) * LANES, LANES)
                turned.append(pltpu.roll(doubled[f, :, pl.ds(at, LANES)], turn, 1))
            for t in range(tiles):
                term = weight * jnp.where(keep, turned[t], turned[t + 1])
                sums[t] = term if sums[t] is None else sums[t] + term
        for t in range(tiles):
            out_ref[0, f, :, t * LANES:(t + 1) * LANES] = sums[t]


def rows_of(bands, lat_t, lon_t, shift, departure_row, extents, table, area, fields, halo):
    rows, field_count, levels, lon_count = fields.shape
    smem = pl.BlockSpec(memory_space=pltpu.SMEM)
    return pl.pallas_call(
        functools.partial(row_kernel, bands),
        grid=(rows,),
        out_shape=jax.ShapeDtypeStruct(fields.shape, fields.dtype),
        in_specs=[smem] * 5 + [pl.BlockSpec(memory_space=pltpu.VMEM)] * 2 + [pl.BlockSpec(memory_space=pl.ANY)] * 2,
        out_specs=pl.BlockSpec((1, field_count, levels, lon_count), lambda r: (r, 0, 0, 0)),
        scratch_shapes=[
            pltpu.VMEM((DEPTH, 4, field_count, levels, lon_count), jnp.float32),
            pltpu.VMEM((field_count, levels, 2 * lon_count), jnp.float32),
            pltpu.VMEM((field_count, levels, LANES), jnp.float32),
            pltpu.SemaphoreType.DMA((DEPTH, 4)),
        ],
        compiler_params=pltpu.CompilerParams(dimension_semantics=("arbitrary",)),
        name="rows",
    )(lat_t, lon_t, shift, departure_row, extents, table, area, fields, halo)


def per_device(fields, lat_fraction, lon_fraction, lon_shift, departure_row, extents):
    bands = lax.axis_size("lat")
    total_rows = bands * fields.shape[0]
    row_ids = np.arange(-(-total_rows // LANES) * LANES)
    area = np.where(row_ids < total_rows, np.cos(math.pi * (row_ids + 0.5) / total_rows - math.pi / 2.0), 0.0)
    area = jnp.asarray(area, jnp.float32)
    halo, table = exchange(lat_fraction, lon_fraction, departure_row, extents, area, fields)
    return rows_of(
        bands, lat_fraction, lon_fraction, lon_shift, departure_row, extents, table, area[None, :], fields, halo
    )


def solution(mesh):
    return jax.shard_map(
        per_device,
        mesh=mesh,
        in_specs=(
            P("lat", None, "lev", None),
            P("lat"),
            P("lat"),
            P("lat"),
            P("lat"),
            P("lat", None),
        ),
        out_specs=P("lat", None, "lev", None),
        check_vma=False,
    )
```

time: 186 us -> 140 us (0.75)
  blocking collectives: 42 us -> 0 us
  Pallas kernels: 134 us -> 140 us
  other arithmetic: 5.41 us -> 0 us
  local copies, waits for them, and re-layouts: 2.78 us -> 0 us
    psum x1 -> x0, blocking collectives: 42 us -> none  [per_device(): lax.psum(jnp.concatenate([placed, taken[None, :]], axis=0), ('lat', 'lev'))]
    pallas_call x2, Pallas kernels: 134 us -> 140 us  [the longest x1 131 us: exchange(): pl.pallas_call(functools.partial(exchange_kernel, bands, levs), out_shape...]
    reduce_sum x3 -> x0, other arithmetic: 2.1 us -> none  [the longest x1 1.91 us: per_device(): sums = jnp.sum(fields, axis=(2, 3))]
where the time goes in v2:
time: 140 us
  Pallas kernels  140 us (100%)
    pallas_call x1, Pallas kernels, exchange(): pl.pallas_call(functools.partial(exchange_kernel, bands, levs), out_shape...  131 us
    pallas_call x1, Pallas kernels, rows_of(): pl.pallas_call(functools.partial(row_kernel, bands), grid=(rows,), out_sh...  8.82 us

profile of v2, /device:TPU:0, one launch (start us, length us, event | category | flops | bytes accessed | tf_op | source)
XLA Modules:
  0.0 139.6 jit_solution(14625166780746796191)
XLA Ops:
  0.0 130.8 %exchange.1 = (f32[80,3,8,2560]{3,2,1,0:T(8,128)}, f32[8,256]{1,0:T(8,128)}) custom-call(f32[10]{0:T(128)} %lat_t_ref.3, f32[10]{0:T(128)} %lon_t_ref.3, s32[10]{0:T(128)} %departure_ref.3, s32[1,2]{1,0:T(1,128)} %extents_ref.3, f32[256]{0:T(256)} %constant.2.clone.area_ref, f32[10,3,8,2560]{3,2,1,0:T(8,128)} %fields_ref.3), custom_call_target="tpu_custom_call" | custom-call | tf_op jit(solution)/shard_map/exchange/pallas_call | solution.py:232
  130.8 8.8 %rows.1 = f32[10,3,8,2560]{3,2,1,0:T(8,128)} custom-call(f32[10]{0:T(128)} %lat_t_ref.3, f32[10]{0:T(128)} %lon_t_ref.3, s32[10]{0:T(128)} %shift_ref.1, s32[10]{0:T(128)} %departure_ref.3, s32[1,2]{1,0:T(1,128)} %extents_ref.3, f32[8,256]{1,0:T(8,128)} %get-tuple-element.7.table_ref, f32[1,256]{1,0:T(1,128)} %constant.9.area_ref, ...), custom_call_target="tpu_custom_call" | custom-call | tf_op jit(solution)/shard_map/rows/pallas_call | solution.py:330

commit v3 on v2

--- a/solution.py
+++ b/solution.py
@@ -11,7 +11,7 @@
 
 REACH = 4
 LANES = 128
-DEPTH = 3
+DEPTH = 10
 MESH = pl.DeviceIdType.MESH
 
 UP = {
@@ -260,10 +260,11 @@
     row_count = pl.num_programs(0)
     rows, field_count, _, lon_count = fields_ref.shape
     tiles = lon_count // LANES
+    depth = held.shape[0]
     first_row = lax.axis_index("lat") * rows
 
     def fetch(index):
-        slot = lax.rem(index, DEPTH)
+        slot = lax.rem(index, depth)
         departure = departure_of(index, first_row, rows, bands * rows, departure_ref, extents_ref)
         start = departure - 1 - (first_row - REACH * rows)
         for a in range(4):
@@ -282,7 +283,7 @@
 
     @pl.when(row == 0)
     def _():
-        for index in range(min(DEPTH - 1, rows)):
+        for index in range(min(depth - 1, rows)):
             fetch(index)
         weight = table_ref[field_count:field_count + 1, :]
         for f in range(field_count):
@@ -291,37 +292,45 @@
             after = jnp.sum(total * weight, axis=1, keepdims=True)
             ratio[f] = jnp.broadcast_to(before / after, ratio.shape[1:])
 
-    @pl.when(row + DEPTH - 1 < row_count)
+    @pl.when(row + depth - 1 < row_count)
     def _():
-        fetch(row + DEPTH - 1)
-
-    slot = lax.rem(row, DEPTH)
+        fetch(row + depth - 1)
+
+    slot = lax.rem(row, depth)
     for a in range(4):
         pltpu.make_async_copy(fields_ref.at[0], held.at[slot, a], sem.at[slot, a]).wait()
     lat_w, lon_w = cubic(lat_t_ref[row]), cubic(lon_t_ref[row])
     lane = lax.broadcasted_iota(jnp.int32, (out_ref.shape[2], LANES), 1)
+    first = lax.rem(shift_ref[row] - 1 + lon_count, lon_count)
+    whole, rest = first // LANES, lax.rem(first, LANES)
+    turn = lax.rem(LANES - rest, LANES)
+    keep = lane < LANES - rest
+
+    def ahead(pieces, step):
+        turned = [pltpu.roll(piece, LANES - step, 1) for piece in pieces]
+        return [jnp.where(lane < LANES - step, turned[t], turned[(t + 1) % tiles]) for t in range(tiles)]
+
     for f in range(field_count):
-        column = lat_w[0] * held[slot, 0, f]
-        for a in range(1, 4):
-            column = column + lat_w[a] * held[slot, a, f]
-        doubled[f, :, 0:lon_count] = column
-        doubled[f, :, lon_count:2 * lon_count] = column
-        sums = [None] * tiles
-        for k in range(4):
-            first = lax.rem(shift_ref[row] + k - 1 + lon_count, lon_count)
-            whole, rest = first // LANES, lax.rem(first, LANES)
-            turn = lax.rem(LANES - rest, LANES)
-            keep = lane < LANES - rest
-            weight = lon_w[k] * ratio[f]
-            turned = []
-            for t in range(tiles + 1):
-                at = pl.multiple_of((whole + t) * LANES, LANES)
-                turned.append(pltpu.roll(doubled[f, :, pl.ds(at, LANES)], turn, 1))
-            for t in range(tiles):
-                term = weight * jnp.where(keep, turned[t], turned[t + 1])
-                sums[t] = term if sums[t] is None else sums[t] + term
+        lon = [weight * ratio[f] for weight in lon_w]
+        column = []
         for t in range(tiles):
-            out_ref[0, f, :, t * LANES:(t + 1) * LANES] = sums[t]
+            at = pl.ds(t * LANES, LANES)
+            total = lat_w[0] * held[slot, 0, f, :, at]
+            for a in range(1, 4):
+                total = total + lat_w[a] * held[slot, a, f, :, at]
+            column.append(total)
+        after = ahead(column, 1)
+        later = ahead([lon[2] * column[t] + lon[3] * after[t] for t in range(tiles)], 2)
+        for t in range(tiles):
+            mixed = lon[0] * column[t] + lon[1] * after[t] + later[t]
+            doubled[f, :, t * LANES:(t + 1) * LANES] = mixed
+            doubled[f, :, lon_count + t * LANES:lon_count + (t + 1) * LANES] = mixed
+        turned = []
+        for t in range(tiles + 1):
+            at = pl.multiple_of((whole + t) * LANES, LANES)
+            turned.append(pltpu.roll(doubled[f, :, pl.ds(at, LANES)], turn, 1))
+        for t in range(tiles):
+            out_ref[0, f, :, t * LANES:(t + 1) * LANES] = jnp.where(keep, turned[t], turned[t + 1])
 
 
 def rows_of(bands, lat_t, lon_t, shift, departure_row, extents, table, area, fields, halo):

time: 140 us -> 140 us (level)
  no operation moved by 1% of the time
where the time goes in v3:
time: 140 us; the launch traced here: 139 us
  Pallas kernels  139 us (99%)
    pallas_call x1, Pallas kernels, exchange(): pl.pallas_call(functools.partial(exchange_kernel, bands, levs), out_shape...  131 us
    pallas_call x1, Pallas kernels, rows_of(): pl.pallas_call(functools.partial(row_kernel, bands), grid=(rows,), out_sh...  8.68 us

profile of v3, /device:TPU:0, one launch (start us, length us, event | category | flops | bytes accessed | tf_op | source)
XLA Modules:
  0.0 139.5 jit_solution(2180888007147355405)
XLA Ops:
  0.0 130.8 %exchange.1 = (f32[80,3,8,2560]{3,2,1,0:T(8,128)}, f32[8,256]{1,0:T(8,128)}) custom-call(f32[10]{0:T(128)} %lat_t_ref.3, f32[10]{0:T(128)} %lon_t_ref.3, s32[10]{0:T(128)} %departure_ref.3, s32[1,2]{1,0:T(1,128)} %extents_ref.3, f32[256]{0:T(256)} %constant.2.clone.area_ref, f32[10,3,8,2560]{3,2,1,0:T(8,128)} %fields_ref.3), custom_call_target="tpu_custom_call" | custom-call | tf_op jit(solution)/shard_map/exchange/pallas_call | solution.py:232
  130.8 8.7 %rows.1 = f32[10,3,8,2560]{3,2,1,0:T(8,128)} custom-call(f32[10]{0:T(128)} %lat_t_ref.3, f32[10]{0:T(128)} %lon_t_ref.3, s32[10]{0:T(128)} %shift_ref.1, s32[10]{0:T(128)} %departure_ref.3, s32[1,2]{1,0:T(1,128)} %extents_ref.3, f32[8,256]{1,0:T(8,128)} %get-tuple-element.7.table_ref, f32[1,256]{1,0:T(1,128)} %constant.9.area_ref, ...), custom_call_target="tpu_custom_call" | custom-call | tf_op jit(solution)/shard_map/rows/pallas_call | solution.py:339

commit v4 on v3

--- a/solution.py
+++ b/solution.py
@@ -11,7 +11,7 @@
 
 REACH = 4
 LANES = 128
-DEPTH = 10
+DEPTH = 5
 MESH = pl.DeviceIdType.MESH
 
 UP = {
@@ -267,19 +267,29 @@
         slot = lax.rem(index, depth)
         departure = departure_of(index, first_row, rows, bands * rows, departure_ref, extents_ref)
         start = departure - 1 - (first_row - REACH * rows)
-        for a in range(4):
-            place = start + a
-            own = jnp.logical_and(place >= REACH * rows, place < (REACH + 1) * rows)
-            target = held.at[slot, a]
-
-            @pl.when(own)
-            def _():
-                pltpu.make_async_copy(fields_ref.at[place - REACH * rows], target, sem.at[slot, a]).start()
-
-            @pl.when(jnp.logical_not(own))
-            def _():
-                away = jnp.where(place < REACH * rows, place, place - rows)
-                pltpu.make_async_copy(halo_ref.at[away], target, sem.at[slot, a]).start()
+        low, high = REACH * rows, (REACH + 1) * rows
+        outside = jnp.logical_or(start + 4 <= low, start >= high)
+
+        @pl.when(outside)
+        def _():
+            away = jnp.where(start < low, start, start - rows)
+            pltpu.make_async_copy(halo_ref.at[pl.ds(away, 4)], held.at[slot], sem.at[slot]).start()
+
+        @pl.when(jnp.logical_not(outside))
+        def _():
+            for a in range(4):
+                place = start + a
+                own = jnp.logical_and(place >= low, place < high)
+                target = held.at[slot, a]
+
+                @pl.when(own)
+                def _():
+                    pltpu.make_async_copy(fields_ref.at[place - low], target, sem.at[slot]).start()
+
+                @pl.when(jnp.logical_not(own))
+                def _():
+                    away = jnp.where(place < low, place, place - rows)
+                    pltpu.make_async_copy(halo_ref.at[away], target, sem.at[slot]).start()
 
     @pl.when(row == 0)
     def _():
@@ -297,8 +307,7 @@
         fetch(row + depth - 1)
 
     slot = lax.rem(row, depth)
-    for a in range(4):
-        pltpu.make_async_copy(fields_ref.at[0], held.at[slot, a], sem.at[slot, a]).wait()
+    pltpu.make_async_copy(halo_ref.at[pl.ds(0, 4)], held.at[slot], sem.at[slot]).wait()
     lat_w, lon_w = cubic(lat_t_ref[row]), cubic(lon_t_ref[row])
     lane = lax.broadcasted_iota(jnp.int32, (out_ref.shape[2], LANES), 1)
     first = lax.rem(shift_ref[row] - 1 + lon_count, lon_count)
@@ -346,7 +355,7 @@
             pltpu.VMEM((DEPTH, 4, field_count, levels, lon_count), jnp.float32),
             pltpu.VMEM((field_count, levels, 2 * lon_count), jnp.float32),
             pltpu.VMEM((field_count, levels, LANES), jnp.float32),
-            pltpu.SemaphoreType.DMA((DEPTH, 4)),
+            pltpu.SemaphoreType.DMA((DEPTH,)),
         ],
         compiler_params=pltpu.CompilerParams(dimension_semantics=("arbitrary",)),
         name="rows",

time: 140 us -> 139 us (level)
  no operation moved by 1% of the time
where the time goes in v4:
time: 139 us
  Pallas kernels  139 us (100%)
    pallas_call x1, Pallas kernels, exchange(): pl.pallas_call(functools.partial(exchange_kernel, bands, levs), out_shape...  131 us
    pallas_call x1, Pallas kernels, rows_of(): pl.pallas_call(functools.partial(row_kernel, bands), grid=(rows,), out_sh...  8.31 us

profile of v4, /device:TPU:0, one launch (start us, length us, event | category | flops | bytes accessed | tf_op | source)
XLA Modules:
  0.0 139.1 jit_solution(7545594031537522428)
XLA Ops:
  0.0 130.8 %exchange.1 = (f32[80,3,8,2560]{3,2,1,0:T(8,128)}, f32[8,256]{1,0:T(8,128)}) custom-call(f32[10]{0:T(128)} %lat_t_ref.3, f32[10]{0:T(128)} %lon_t_ref.3, s32[10]{0:T(128)} %departure_ref.3, s32[1,2]{1,0:T(1,128)} %extents_ref.3, f32[256]{0:T(256)} %constant.2.clone.area_ref, f32[10,3,8,2560]{3,2,1,0:T(8,128)} %fields_ref.3), custom_call_target="tpu_custom_call" | custom-call | tf_op jit(solution)/shard_map/exchange/pallas_call | solution.py:232
  130.8 8.3 %rows.1 = f32[10,3,8,2560]{3,2,1,0:T(8,128)} custom-call(f32[10]{0:T(128)} %lat_t_ref.3, f32[10]{0:T(128)} %lon_t_ref.3, s32[10]{0:T(128)} %shift_ref.1, s32[10]{0:T(128)} %departure_ref.3, s32[1,2]{1,0:T(1,128)} %extents_ref.3, f32[8,256]{1,0:T(8,128)} %get-tuple-element.7.table_ref, f32[1,256]{1,0:T(1,128)} %constant.9.area_ref, ...), custom_call_target="tpu_custom_call" | custom-call | tf_op jit(solution)/shard_map/rows/pallas_call | solution.py:348
